TPU v7x, 32 devices: a whole 2x2x4 slice. The times are simulated.
32 devices in a mesh: seq: 8 (over z, y), grp: 4 (over x, core).
Axes of the slice: x: 2, y: 2, z: 4, core: 2. Of those that a mesh axis runs over, the one named last changes fastest.
Arguments:
- tokens: bfloat16 [4096, 2560], P('seq'), may hold values from -6 to 6
- norm_gain: float32 [2560], replicated, may hold values from 0.25 to 1.75
- inner_weight: bfloat16 [2560, 2, 5120], P(None, None, ('grp', 'seq')), may hold values from -0.125 to 0.125
- state_weight: bfloat16 [2560, 2, 128], replicated, may hold values from -0.125 to 0.125
- step_weight: bfloat16 [2560, 80], P(None, 'grp'), may hold values from -0.125 to 0.125
- step_bias: float32 [80], P('grp'), may hold values from -1 to 1
- decay_rate: float32 [80], P('grp'), may hold values from 4.8828124e-06 to 0.05
- skip_scale: float32 [80], P('grp'), may hold values from 0.5 to 1.5
- conv_inner: bfloat16 [4, 5120], P(None, 'grp'), may hold values from -3 to 3
- conv_state: bfloat16 [4, 2, 128], replicated, may hold values from -3 to 3
- out_gain: float32 [5120], P('grp'), may hold values from 0.25 to 1.75
- out_weight: bfloat16 [5120, 2560], P(None, 'grp'), may hold values from -0.078125 to 0.078125
Outputs:
- mixed: bfloat16 [4096, 2560], P('seq', 'grp')
All inputs are finite; a program needn't handle non-finite values.
Results may differ from a plain program's by a relative error of at most 0.0075.
Values may be sent and summed in bfloat16 or wider, within the bound.
No kernel may reach another device: no remote copies, remote signals or barrier semaphores. Data moves between devices by JAX's collectives and lax.ppermute only.
A program may use at most 64 MiB of HBM per device.

v0:
```python
from functools import partial
import jax
import jax.numpy as jnp
from jax import lax
from jax.sharding import PartitionSpec as P

SPAN = 256
EPS = 1e-05
HIGH = lax.Precision.HIGHEST


def from_behind(value, axis, steps):
    count = lax.axis_size(axis)
    leading, last = (max(0, -steps), min(count, count - steps))
    return lax.ppermute(value, axis, [(source, source + steps) for source in range(leading, last)])


def prefix(value, axis, combine, identity):
    length, place = (lax.axis_size(axis), lax.axis_index(axis))
    everything = jax.tree.map(lambda part: lax.all_gather(part, axis), value)
    start = jax.tree.map(
        lambda part, zero: jnp.broadcast_to(jnp.asarray(zero, part.dtype), part.shape),
        value,
        identity,
    )

    def step(k, before):
        reached = k < place
        new = combine(before, jax.tree.map(lambda part: part[k], everything))
        return jax.tree.map(lambda a, b: jnp.where(reached, a, b), new, before)

    return lax.fori_loop(0, length, step, start)


def conv_rows(before, current, weight):
    width = weight.shape[0]
    padded = jnp.concatenate([before, current], axis=0).astype(jnp.float32)
    length = current.shape[0]
    total = jnp.zeros(current.shape, jnp.float32)
    for offset in range(width):
        total = total + weight[offset].astype(jnp.float32) * padded[offset : offset + length]
    return jax.nn.silu(total).astype(jnp.bfloat16)


def span_step(rate, skip, state, inputs):
    xvals, bmat, cmat, delta = inputs
    logdec = -delta * rate[None, :]
    cumul = jnp.cumsum(logdec, axis=0)
    length = cumul.shape[0]
    scores = jnp.einsum("tn,sn->ts", cmat, bmat, preferred_element_type=jnp.float32)
    lower = jnp.arange(length)[:, None] >= jnp.arange(length)[None, :]
    diffs = cumul.T[:, :, None] - cumul.T[:, None, :]
    decay = jnp.exp(jnp.where(lower[None], diffs, -jnp.inf))
    mixer = (scores[None] * decay * delta.T[:, None, :]).astype(jnp.bfloat16)
    intra = jnp.einsum("hts,shp->thp", mixer, xvals, preferred_element_type=jnp.float32)
    inter = jnp.exp(cumul)[:, :, None] * jnp.einsum(
        "tn,hpn->thp", cmat.astype(jnp.float32), state, precision=HIGH
    )
    output = intra + inter + skip[None, :, None] * xvals.astype(jnp.float32)
    tail = jnp.exp(cumul[-1][None, :] - cumul) * delta
    weighted = (tail[:, :, None] * bmat.astype(jnp.float32)[:, None, :]).astype(jnp.bfloat16)
    update = jnp.einsum("shp,shn->hpn", xvals, weighted, preferred_element_type=jnp.float32)
    new_state = jnp.exp(cumul[-1])[:, None, None] * state + update
    return (new_state, output)


def body(
    tokens,
    norm_gain,
    inner_weight,
    state_weight,
    step_weight,
    step_bias,
    decay_rate,
    skip_scale,
    conv_inner,
    conv_state,
    out_gain,
    out_weight,
):
    tok_rows = tokens.shape[0]
    model_width = tokens.shape[1]
    wide = tokens.astype(jnp.float32)
    normed = (
        wide * lax.rsqrt(jnp.mean(wide * wide, axis=1, keepdims=True) + EPS) * norm_gain
    ).astype(jnp.bfloat16)
    piece = lax.all_gather(inner_weight, "seq", axis=2, tiled=True)
    count = piece.shape[2]
    flat = piece.reshape(piece.shape[0], 2 * count)
    result = jnp.dot(normed, flat, preferred_element_type=jnp.float32).astype(jnp.bfloat16)
    inner = result.reshape(tok_rows, 2, count)
    state_flat = state_weight.reshape(model_width, -1)
    state_pre = (
        jnp.dot(normed, state_flat, preferred_element_type=jnp.float32)
        .astype(jnp.bfloat16)
        .reshape(tok_rows, 2, -1)
    )
    delta = jax.nn.softplus(
        jnp.dot(normed, step_weight, preferred_element_type=jnp.float32) + step_bias
    )
    inner_values = inner[:, 0, :]
    width = conv_inner.shape[0]
    first_kept = tok_rows - width + 1
    before_values, before_state = from_behind(
        (inner_values[first_kept:], state_pre[first_kept:]), "seq", 1
    )
    values = conv_rows(before_values, inner_values, conv_inner)
    conv_out = conv_rows(before_state, state_pre, conv_state)
    heads_here = delta.shape[1]
    head_width = values.shape[1] // heads_here
    state_width = conv_out.shape[2]
    blocks = tok_rows // SPAN
    xs_blocks = values.reshape(blocks, SPAN, heads_here, head_width)
    b_blocks = conv_out[:, 0, :].reshape(blocks, SPAN, state_width)
    c_blocks = conv_out[:, 1, :].reshape(blocks, SPAN, state_width)
    d_blocks = delta.reshape(blocks, SPAN, heads_here)
    initial = jnp.zeros((heads_here, head_width, state_width), jnp.float32)
    final_state, outputs = lax.scan(
        partial(span_step, decay_rate, skip_scale),
        initial,
        (xs_blocks, b_blocks, c_blocks, d_blocks),
    )
    cumdev = jnp.cumsum(-delta * decay_rate[None, :], axis=0)
    totals = cumdev[-1]

    def combine(earlier, later):
        return (earlier[0] + later[0], jnp.exp(later[0])[:, None, None] * earlier[1] + later[1])

    scanned = prefix(
        (totals, final_state), "seq", combine, (jnp.zeros_like(totals), jnp.zeros_like(final_state))
    )
    incoming = scanned[1]
    cmat_wide = conv_out[:, 1, :].astype(jnp.float32)
    carried = jnp.exp(cumdev)[:, :, None] * jnp.einsum(
        "tn,hpn->thp", cmat_wide, incoming, precision=HIGH
    )
    mixed_heads = (outputs.reshape(tok_rows, heads_here, head_width) + carried).reshape(
        tok_rows, heads_here * head_width
    )
    gated = mixed_heads * jax.nn.silu(inner[:, 1, :].astype(jnp.float32))
    squares = lax.psum(jnp.sum(gated * gated, axis=1), "grp")
    row_scale = lax.rsqrt(squares / (lax.axis_size("grp") * gated.shape[1]) + EPS)
    scaled = (gated * out_gain).astype(jnp.bfloat16)
    summed = jnp.dot(
        lax.all_gather(scaled, "grp", axis=1, tiled=True),
        out_weight,
        preferred_element_type=jnp.float32,
    )
    return (summed * row_scale[:, None]).astype(jnp.bfloat16)


def solution(mesh):
    return jax.shard_map(
        body,
        mesh=mesh,
        in_specs=(
            P("seq", None),
            P(),
            P(None, None, ("grp", "seq")),
            P(),
            P(None, "grp"),
            P("grp"),
            P("grp"),
            P("grp"),
            P(None, "grp"),
            P(),
            P("grp"),
            P(None, "grp"),
        ),
        out_specs=P("seq", "grp"),
        check_vma=False,
    )
```

profile of v0, /device:TPU:0, one launch (start us, length us, event | category | flops | bytes accessed | tf_op | source)
XLA Modules:
  0.0 453.3 jit_solution(12982020083999643823)
XLA Ops:
  7.3 2.4 fusion.40
  10.8 4.9 %collective-permute-start.1 = (bf16[3,2,128]{2,0,1:T(4,128)(2,1)S(1)}, bf16[3,2,128]{2,0,1:T(4,128)(2,1)S(1)}, u32[]{:S(2)}, u32[]{:S(2)}) collective-permute-start(bf16[3,2,128]{2,0,1:T(4,128)(2,1)S(1)} %slice_bitcast_fusion.2), channel_id=1, source_target_pairs={{0,4},{4,8},{8,12},{12,16},{16,20},{20,24},{24,28},{1,5},{5,9},{9,... | collective-permute-start | bytes 4616 | tf_op jit(solution)/shard_map/ppermute | solution.py:15
  16.4 1.5 compare_select_fusion.1
  20.8 174.0 %all-gather.6.cloned.1.call-done = bf16[2560,2,1280]{0,2,1:T(8,128)(2,1)} async-done(((bf16[2560,2,160]{0,2,1:T(8,128)(2,1)}), bf16[2560,2,1280]{0,2,1:T(8,128)(2,1)}) %all-gather.6.cloned.1.call-update) | async-done | bytes 13107216 | tf_op jit(solution)/shard_map/all_gather | solution.py:87
  194.8 11.2 %convolution_convert_fusion = bf16[512,2560]{1,0:T(8,128)(2,1)} fusion(bf16[2560,2560]{0,1:T(8,128)(2,1)} %bitcast.199, bf16[512,2560]{1,0:T(8,128)(2,1)S(1)} %copy-done.6, f32[2560]{0:T(1024)S(1)} %copy-done.16, f32[512]{0:T(512)S(1)} %add_rsqrt_fusion.1), kind=kOutput, calls=%fused_computation.59 | convolution fusion | flops 6717440000 | bytes 18362368 | tf_op jit(solution)/shard_map/dot_general | solution.py:90
  206.0 3.0 copy.65
  209.1 2.6 collective-permute-start
  211.8 2.0 slice_convert_fusion
  213.8 4.0 collective-permute-done
  218.5 3.2 multiply_convert_fusion.8
  222.4 71.2 %while.27 = (s32[]{:T(128)}, f32[20,64,128]{2,1,0:T(8,128)S(1)}, f32[2,256,20,64]{1,0,3,2:T(2,128)}, f32[2,256,20]{1,0,2:T(2,128)S(1)}, f32[20]{0:T(128)S(1)}, /...) while((s32[]{:T(128)}, f32[20,64,128]{2,1,0:T(8,128)S(1)}, ...), condition=%wide.region_4.5_spmd.clone, body=%wide.region_1.4_spmd.clone.sunk | while | flops 782684224 | bytes 15246184 | solution.py:118
  225.2 1.5 fusion.101
  229.1 27.0 %dynamic_update_slice.6 = f32[2,256,20,64]{1,0,3,2:T(2,128)} dynamic-update-slice(f32[2,256,20,64]{1,0,3,2:T(2,128)} %get-tuple-element.384, f32[1,256,20,64]{1,0,3,2:T(1,128)S(1)} %copy.106, s32[]{:T(128)} %get-tuple-element.382, s32[]{:T(128)} %constant.66.clone.1..sunk, s32[]{:T(128)} %constant.66.clone.1..sunk, s32[]{:T(128)} %constant.66.clone.1..sunk) | dynamic-update-slice | bytes 2621444 | tf_op jit(solution)/shard_map/while/body/jit(dynamic_update_index_in_dim)/dynamic_update_slice | solution.py:118
  260.8 1.5 fusion.101
  264.7 27.0 %dynamic_update_slice.6 = f32[2,256,20,64]{1,0,3,2:T(2,128)} dynamic-update-slice(f32[2,256,20,64]{1,0,3,2:T(2,128)} %get-tuple-element.384, f32[1,256,20,64]{1,0,3,2:T(1,128)S(1)} %copy.106, s32[]{:T(128)} %get-tuple-element.382, s32[]{:T(128)} %constant.66.clone.1..sunk, s32[]{:T(128)} %constant.66.clone.1..sunk, s32[]{:T(128)} %constant.66.clone.1..sunk) | dynamic-update-slice | bytes 2621444 | tf_op jit(solution)/shard_map/while/body/jit(dynamic_update_index_in_dim)/dynamic_update_slice | solution.py:118
  297.2 21.1 %all-gather.1 = f32[8,1,20]{2,1,0:T(1,128)S(1)} all-gather(f32[1,1,20]{2,1,0:T(1,128)S(1)} %bitcast.198), channel_id=1, replica_groups=mesh['seq'=8,'grp'=4] {'seq'}, dimensions={0}, use_global_device_ids=true | all-gather | bytes 720 | tf_op jit(solution)/shard_map/all_gather | solution.py:20
  318.3 4.9 %reshape.128 = f32[512,20,64]{0,2,1:T(8,128)} reshape(f32[2,256,20,64]{1,0,3,2:T(2,128)} %get-tuple-element.147) | data formatting | bytes 5242880 | tf_op jit(solution)/shard_map/reshape | solution.py:137
  323.2 59.1 %all-gather.10.cloned.1.call-done = f32[160,64,128]{2,1,0:T(8,128)} async-done(((f32[20,64,128]{2,1,0:T(8,128)}), f32[160,64,128]{2,1,0:T(8,128)}) %all-gather.10.cloned.1.call-update) | async-done | bytes 5242896 | tf_op jit(solution)/shard_map/all_gather | solution.py:20
  382.3 10.2 %while.28 = (s32[]{:T(128)}, f32[20,64,128]{2,1,0:T(8,128)S(1)}, s32[]{:T(128)}, f32[8,20]{1,0:T(8,128)S(1)}, f32[8,20,64,128]{3,2,1,0:T(8,128)}, /*index=5*/s32[]{:T(128)}, s32[]{:T(128)}) while((s32[]{:T(128)}, f32[20,64,128]{2,1,0:T(8,128)S(1)}, s32[]{:T(128)}, f32[8,20]{1,0:T(8,128)S(1)}, f32[8,20,64,128]{3,2,1,0:T(8,128)}, ...), condition=%wide.region_8.9_spmd.clone, body=%wide.region_7.8_spmd.clone.sunk | while | flops 655364 | bytes 1966425 | solution.py:32
  392.5 3.9 multiply_reduce_fusion
  396.4 2.0 fusion.51
  398.4 5.7 %psum.7 = f32[512]{0:T(512)S(1)} all-reduce(f32[512]{0:T(512)S(1)} %get-tuple-element.278), channel_id=1, replica_groups=mesh['seq'=8,'grp'=4] {'grp'}, use_global_device_ids=true, to_apply=%region_10.11 | all-reduce | flops 512 | bytes 4096 | tf_op jit(solution)/shard_map/psum | solution.py:141
  404.1 33.1 %all-gather.8.cloned.1.call-done = bf16[512,5120]{0,1:T(8,128)(2,1)} async-done(((bf16[512,1280]{0,1:T(8,128)(2,1)}), bf16[512,5120]{0,1:T(8,128)(2,1)}) %all-gather.8.cloned.1.call-update) | async-done | bytes 5242896 | tf_op jit(solution)/shard_map/all_gather | solution.py:145
  437.2 9.6 %fusion.52 = bf16[512,640]{1,0:T(8,128)(2,1)} fusion(bf16[512,5120]{0,1:T(8,128)(2,1)} %all-gather.8.cloned.1.call-done, bf16[5120,640]{1,0:T(8,128)(2,1)} %param.27, f32[512]{0:T(512)S(1)} %add_rsqrt_fusion), kind=kOutput, calls=%fused_computation.80 | convolution fusion | flops 3356098560 | bytes 12453888 | tf_op jit(solution)/shard_map/dot_general | solution.py:144
  (138 shorter events, 34.1 us)
Async XLA Ops:
  6.5 9.9 %copy-start = (bf16[2560,20]{0,1:T(8,128)(2,1)S(1)}, bf16[2560,20]{0,1:T(8,128)(2,1)}, u32[]{:S(2)}) copy-start(bf16[2560,20]{0,1:T(8,128)(2,1)} %param.20) | copy-start | bytes 307204
  6.5 3.2 copy-start.6
  6.5 3.2 copy-start.16
  6.5 188.2 %all-gather.6.cloned.1.call-start = ((), (), s32[]{:S(2)}) async-start(), calls=%async_computation | async-start | bytes 14745600 | tf_op jit(solution)/shard_map/all_gather | solution.py:87
  7.3 375.0 %all-gather.10.cloned.1.call-start = ((), (), s32[]{:S(2)}) async-start(), calls=%async_computation.2 | async-start | bytes 5898240 | tf_op jit(solution)/shard_map/all_gather | solution.py:20
  7.3 2.5 copy-start.15
  9.8 5.9 %copy-start.14 = (bf16[4,2,128]{2,1,0:T(2,128)(2,1)S(1)}, bf16[4,2,128]{2,1,0:T(2,128)(2,1)}, u32[]{:S(2)}) copy-start(bf16[4,2,128]{2,1,0:T(2,128)(2,1)} %param.25) | copy-start | bytes 6148
  9.8 6.6 %copy-start.17 = (f32[20]{0:T(128)S(1)}, f32[20]{0:T(128)}, u32[]{:S(2)}) copy-start(f32[20]{0:T(128)} %param.21) | copy-start | bytes 244
  10.8 7.3 %collective-permute-start.1 = (bf16[3,2,128]{2,0,1:T(4,128)(2,1)S(1)}, bf16[3,2,128]{2,0,1:T(4,128)(2,1)S(1)}, u32[]{:S(2)}, u32[]{:S(2)}) collective-permute-start(bf16[3,2,128]{2,0,1:T(4,128)(2,1)S(1)} %slice_bitcast_fusion.2), channel_id=1, source_target_pairs={{0,4},{4,8},{8,12},{12,16},{16,20},{20,24},{24,28},{1,5},{5,9},{9,... | collective-permute-start | bytes 4616 | tf_op jit(solution)/shard_map/ppermute | solution.py:15
  15.7 2.3 copy-start.10
  19.5 0.7 copy-start.7
  209.0 4.8 %copy-start.3 = (bf16[512,2560]{0,1:T(8,128)(2,1)}, bf16[512,2560]{0,1:T(8,128)(2,1)S(1)}, u32[]{:S(2)}) copy-start(bf16[512,2560]{0,1:T(8,128)(2,1)S(1)} %copy.65) | copy-start | bytes 7864324
  209.1 8.7 %collective-permute-start = (bf16[3,1280]{0,1:T(8,128)(2,1)S(1)}, bf16[3,1280]{0,1:T(8,128)(2,1)S(1)}, u32[]{:S(2)}, u32[]{:S(2)}) collective-permute-start(bf16[3,1280]{0,1:T(8,128)(2,1)S(1)} %slice_bitcast_fusion.1), channel_id=1, source_target_pairs={{0,4},{4,8},{8,12},{12,16},{16,20},{20,24},{24,28},{1,5},{5,9},{9,... | collective-permute-start | bytes 23048 | tf_op jit(solution)/shard_map/ppermute | solution.py:15
  221.8 0.7 copy-start.11
  221.8 0.7 copy-start.12
  229.1 28.9 %copy-start.9 = (f32[2,256,20]{1,0,2:T(2,128)S(1)}, f32[2,256,20]{1,0,2:T(2,128)}, u32[]{:S(2)}) copy-start(f32[2,256,20]{1,0,2:T(2,128)} %copy-done.8) | copy-start | bytes 122884 | tf_op jit(solution)/shard_map/while
  258.0 0.6 copy-start.8
  264.7 28.9 %copy-start.9 = (f32[2,256,20]{1,0,2:T(2,128)S(1)}, f32[2,256,20]{1,0,2:T(2,128)}, u32[]{:S(2)}) copy-start(f32[2,256,20]{1,0,2:T(2,128)} %copy-done.8) | copy-start | bytes 122884 | tf_op jit(solution)/shard_map/while
  293.6 0.8 copy-start.2
  294.5 142.7 %all-gather.8.cloned.1.call-start = ((), (), s32[]{:S(2)}) async-start(), calls=%async_computation.1 | async-start | bytes 6553600 | tf_op jit(solution)/shard_map/all_gather | solution.py:145
  318.3 74.2 %copy-start.5 = (f32[512,1,1280]{0,2,1:T(8,128)S(1)}, f32[512,1,1280]{0,2,1:T(8,128)}, u32[]{:S(2)}) copy-start(f32[512,1,1280]{0,2,1:T(8,128)} %get-tuple-element.268) | copy-start | bytes 7864324
  392.4 4.0 copy-start.4
  392.4 4.0 copy-start.13
  437.2 9.6 %copy-start.1 = (bf16[2560,20]{0,1:T(8,128)(2,1)S(1)}, bf16[2560,20]{0,1:T(8,128)(2,1)}, u32[]{:S(2)}) copy-start(bf16[2560,20]{0,1:T(8,128)(2,1)} %param.20) | copy-start | bytes 307204
  (1 other events, 0.6 us)
Sparse Core Ops, SparseCore 0:
  9.5 185.2 all-gather.5
  294.6 87.5 all-gather.9
  398.5 38.5 all-gather.7
where the time goes:
time: 458 us; the launch traced here: 453 us
  waiting for transfers between devices  271 us (59%)
  local copies, waits for them, and re-layouts  71 us (16%)
  matrix products  35.7 us (8%)
  other arithmetic  27.3 us (6%)
  blocking collectives  26.8 us (6%)
  between operations  13.5 us (3%)
  starting transfers between devices  7.63 us (2%)
    all_gather x1, waiting for transfers between devices, body(): piece = lax.all_gather(inner_weight, 'seq', axis=2, tiled=True)  174 us
    all_gather x1, waiting for transfers between devices, prefix(): everything = jax.tree.map(lambda part: lax.all_gather(part, axis), value)  59.1 us
    dynamic_update_slice x4, local copies, waits for them, and re-layouts, body(): lax.scan(partial(span_step, decay_rate, skip_scale), initial, (xs_blocks,...  56.8 us
    all_gather x1, waiting for transfers between devices, body(): lax.all_gather(scaled, 'grp', axis=1, tiled=True)  33.1 us
    all_gather x1, blocking collectives, prefix(): everything = jax.tree.map(lambda part: lax.all_gather(part, axis), value)  21.1 us
    dot_general x1, matrix products, body(): jnp.dot(normed, flat, preferred_element_type=jnp.float32)  11.2 us
    select_n x8, other arithmetic, step(): return jax.tree.map(lambda a, b: jnp.where(reached, a, b), new, before)  9.86 us
    dot_general x1, matrix products, body(): jnp.dot(lax.all_gather(scaled, 'grp', axis=1, tiled=True), out_weight, pr...  9.57 us
  transfers between devices with their start and end apart: 5, of which 4 were waited for; matrix products, arithmetic and copies ran while one was open for 4% of the time, Pallas kernels for 0%

commit v1 on v0

--- a/solution.py
+++ b/solution.py
@@ -84,7 +84,22 @@
     normed = (
         wide * lax.rsqrt(jnp.mean(wide * wide, axis=1, keepdims=True) + EPS) * norm_gain
     ).astype(jnp.bfloat16)
-    piece = lax.all_gather(inner_weight, "seq", axis=2, tiled=True)
+    ways, here, step_2 = (lax.axis_size("seq"), lax.axis_index("seq"), inner_weight.shape[2])
+    shape = [n * ways if d == 2 else n for d, n in enumerate(inner_weight.shape)]
+    piece = lax.dynamic_update_slice_in_dim(
+        jnp.zeros(shape, inner_weight.dtype), inner_weight, here * step_2, axis=2
+    )
+    going_up = going_down = inner_weight
+    for far in range(1, ways // 2 + 1):
+        going_up = lax.ppermute(going_up, "seq", [(d, (d + 1) % ways) for d in range(ways)])
+        piece = lax.dynamic_update_slice_in_dim(
+            piece, going_up, (here - far) % ways * step_2, axis=2
+        )
+        if 2 * far < ways:
+            going_down = lax.ppermute(going_down, "seq", [(d, (d - 1) % ways) for d in range(ways)])
+            piece = lax.dynamic_update_slice_in_dim(
+                piece, going_down, (here + far) % ways * step_2, axis=2
+            )
     count = piece.shape[2]
     flat = piece.reshape(piece.shape[0], 2 * count)
     result = jnp.dot(normed, flat, preferred_element_type=jnp.float32).astype(jnp.bfloat16)

time: 458 us -> 524 us (1.14)
  waiting for transfers between devices: 271 us -> 296 us
  local copies, waits for them, and re-layouts: 71 us -> 93.6 us
  starting transfers between devices: 7.63 us -> 23.1 us
    ppermute x0 -> x7, waiting for transfers between devices: none -> 203 us  [the longest x4 202 us: body(): lax.ppermute(going_up, 'seq', [(d, (d + 1) % ways) for d in range(ways)])]
    all_gather x1 -> x0, waiting for transfers between devices: 174 us -> none  [body(): piece = lax.all_gather(inner_weight, 'seq', axis=2, tiled=True)]
    ppermute x0 -> x7, starting transfers between devices: none -> 19 us  [the longest x4 10.4 us: body(): lax.ppermute(going_up, 'seq', [(d, (d + 1) % ways) for d in range(ways)])]
    dynamic_update_slice x0 -> x8, local copies, waits for them, and re-layouts: none -> 17.6 us  [the longest x4 8.02 us: body(): lax.dynamic_update_slice_in_dim(piece, going_up, (here - far) % ways * st...]
    broadcast_in_dim x0 -> x1, local copies, waits for them, and re-layouts: none -> 5.51 us  [body(): jnp.zeros(shape, inner_weight.dtype)]
  transfers between devices with their start and end apart: 5 -> 11, of which waited for: 4 -> 7; matrix products, arithmetic and copies ran while one was open for 4% -> 8% of each run, Pallas kernels for 0% -> 0%
where the time goes in v1:
time: 524 us; the launch traced here: 519 us
  waiting for transfers between devices  296 us (56%)
  local copies, waits for them, and re-layouts  93.6 us (18%)
  matrix products  37.1 us (7%)
  blocking collectives  27.5 us (5%)
  other arithmetic  27.3 us (5%)
  starting transfers between devices  23.1 us (4%)
  between operations  13.9 us (3%)
    ppermute x4, waiting for transfers between devices, body(): lax.ppermute(going_up, 'seq', [(d, (d + 1) % ways) for d in range(ways)])  202 us
    all_gather x1, waiting for transfers between devices, prefix(): everything = jax.tree.map(lambda part: lax.all_gather(part, axis), value)  58.2 us
    dynamic_update_slice x4, local copies, waits for them, and re-layouts, body(): lax.scan(partial(span_step, decay_rate, skip_scale), initial, (xs_blocks,...  56.8 us
    all_gather x1, waiting for transfers between devices, body(): lax.all_gather(scaled, 'grp', axis=1, tiled=True)  33.1 us
    all_gather x1, blocking collectives, prefix(): everything = jax.tree.map(lambda part: lax.all_gather(part, axis), value)  21.9 us
    dot_general x1, matrix products, body(): jnp.dot(normed, flat, preferred_element_type=jnp.float32)  11.2 us
  transfers between devices with their start and end apart: 11, of which 7 were waited for; matrix products, arithmetic and copies ran while one was open for 8% of the time, Pallas kernels for 0%

profile of v1, /device:TPU:0, one launch (start us, length us, event | category | flops | bytes accessed | tf_op | source)
XLA Modules:
  0.0 519.1 jit_solution(16606516852513915350)
XLA Ops:
  6.5 3.0 collective-permute-start
  9.5 3.1 collective-permute-start.1
  12.6 67.4 %collective-permute-done = bf16[2560,2,160]{0,2,1:T(8,128)(2,1)S(1)} collective-permute-done((bf16[2560,2,160]{0,2,1:T(8,128)(2,1)}, bf16[2560,2,160]{0,2,1:T(8,128)(2,1)S(1)}, u32[]{:S(2)}, u32[]{:S(2)}) %collective-permute-start) | collective-permute-done | bytes 1638432 | tf_op jit(solution)/shard_map/ppermute | solution.py:94
  93.6 58.1 %collective-permute-done.2 = bf16[2560,2,160]{0,2,1:T(8,128)(2,1)} collective-permute-done((bf16[2560,2,160]{0,2,1:T(8,128)(2,1)S(1)}, bf16[2560,2,160]{0,2,1:T(8,128)(2,1)}, u32[]{:S(2)}, u32[]{:S(2)}) %collective-permute-start.2) | collective-permute-done | bytes 1638432 | tf_op jit(solution)/shard_map/ppermute | solution.py:94
  155.2 5.5 %broadcast_in_dim.18 = bf16[2560,2,1280]{0,2,1:T(8,128)(2,1)} broadcast(bf16[]{:T(256)} %constant.115.clone.1), dimensions={} | broadcast | bytes 13107202 | tf_op jit(solution)/shard_map/broadcast_in_dim | solution.py:90
  160.7 2.8 constant_dynamic-update-slice_fusion.7
  165.8 3.1 collective-permute-start.5
  170.3 52.8 %collective-permute-done.4 = bf16[2560,2,160]{0,2,1:T(8,128)(2,1)} collective-permute-done((bf16[2560,2,160]{0,2,1:T(8,128)(2,1)}, bf16[2560,2,160]{0,2,1:T(8,128)(2,1)}, u32[]{:S(2)}, u32[]{:S(2)}) %collective-permute-start.4) | collective-permute-done | bytes 1638432 | tf_op jit(solution)/shard_map/ppermute | solution.py:94
  231.0 2.8 constant_dynamic-update-slice_fusion.3
  237.8 24.2 %collective-permute-done.6 = bf16[2560,2,160]{0,2,1:T(8,128)(2,1)S(1)} collective-permute-done((bf16[2560,2,160]{0,2,1:T(8,128)(2,1)}, bf16[2560,2,160]{0,2,1:T(8,128)(2,1)S(1)}, u32[]{:S(2)}, u32[]{:S(2)}) %collective-permute-start.6) | collective-permute-done | bytes 1638432 | tf_op jit(solution)/shard_map/ppermute | solution.py:94
  263.3 11.2 %convolution_convert_fusion = bf16[512,2560]{1,0:T(8,128)(2,1)} fusion(bf16[2560,2560]{0,1:T(8,128)(2,1)} %bitcast.185, bf16[512,2560]{1,0:T(8,128)(2,1)S(1)} %copy-done.6, f32[2560]{0:T(1024)S(1)} %copy-done.17, f32[512]{0:T(512)S(1)} %add_rsqrt_fusion.1), kind=kOutput, calls=%fused_computation.59 | convolution fusion | flops 6717440000 | bytes 18362368 | tf_op jit(solution)/shard_map/dot_general | solution.py:105
  274.5 3.0 copy.65
  284.2 3.2 multiply_convert_fusion.8
  288.1 71.2 %while.27 = (s32[]{:T(128)}, f32[20,64,128]{2,1,0:T(8,128)S(1)}, f32[2,256,20,64]{1,0,3,2:T(2,128)}, f32[2,256,20]{1,0,2:T(2,128)S(1)}, f32[20]{0:T(128)S(1)}, /...) while((s32[]{:T(128)}, f32[20,64,128]{2,1,0:T(8,128)S(1)}, ...), condition=%wide.region_4.5_spmd.clone, body=%wide.region_1.4_spmd.clone.sunk | while | flops 782684224 | bytes 15246184 | solution.py:133
  294.8 27.0 %dynamic_update_slice.46 = f32[2,256,20,64]{1,0,3,2:T(2,128)} dynamic-update-slice(f32[2,256,20,64]{1,0,3,2:T(2,128)} %get-tuple-element.384, f32[1,256,20,64]{1,0,3,2:T(1,128)S(1)} %copy.106, s32[]{:T(128)} %get-tuple-element.382, s32[]{:T(128)} %constant.111.clone.1..sunk, s32[]{:T(128)} %constant.111.clone.1..sunk, s32[]{:T(128)} %constant.111.clone.1..sunk) | dynamic-update-slice | bytes 2621444 | tf_op jit(solution)/shard_map/while/body/jit(dynamic_update_index_in_dim)/dynamic_update_slice | solution.py:133
  330.4 27.0 %dynamic_update_slice.46 = f32[2,256,20,64]{1,0,3,2:T(2,128)} dynamic-update-slice(f32[2,256,20,64]{1,0,3,2:T(2,128)} %get-tuple-element.384, f32[1,256,20,64]{1,0,3,2:T(1,128)S(1)} %copy.106, s32[]{:T(128)} %get-tuple-element.382, s32[]{:T(128)} %constant.111.clone.1..sunk, s32[]{:T(128)} %constant.111.clone.1..sunk, s32[]{:T(128)} %constant.111.clone.1..sunk) | dynamic-update-slice | bytes 2621444 | tf_op jit(solution)/shard_map/while/body/jit(dynamic_update_index_in_dim)/dynamic_update_slice | solution.py:133
  362.8 21.9 %all-gather.1 = f32[8,1,20]{2,1,0:T(1,128)S(1)} all-gather(f32[1,1,20]{2,1,0:T(1,128)S(1)} %bitcast.199), channel_id=1, replica_groups=mesh['seq'=8,'grp'=4] {'seq'}, dimensions={0}, use_global_device_ids=true | all-gather | bytes 720 | tf_op jit(solution)/shard_map/all_gather | solution.py:20
  384.7 4.9 reshape.128
  389.6 58.2 %all-gather.7.cloned.1.call-done = f32[160,64,128]{2,1,0:T(8,128)} async-done(((f32[20,64,128]{2,1,0:T(8,128)}), f32[160,64,128]{2,1,0:T(8,128)}) %all-gather.7.cloned.1.call-update) | async-done | bytes 5242896 | tf_op jit(solution)/shard_map/all_gather | solution.py:20
  447.8 10.2 %while.28 = (s32[]{:T(128)}, f32[20,64,128]{2,1,0:T(8,128)S(1)}, s32[]{:T(128)}, f32[8,20]{1,0:T(8,128)S(1)}, f32[8,20,64,128]{3,2,1,0:T(8,128)}, /*index=5*/s32[]{:T(128)}, s32[]{:T(128)}) while((s32[]{:T(128)}, f32[20,64,128]{2,1,0:T(8,128)S(1)}, s32[]{:T(128)}, f32[8,20]{1,0:T(8,128)S(1)}, f32[8,20,64,128]{3,2,1,0:T(8,128)}, ...), condition=%wide.region_8.9_spmd.clone, body=%wide.region_7.8_spmd.clone.sunk | while | flops 655364 | bytes 1966425 | solution.py:32
  458.0 3.9 multiply_reduce_fusion
  464.0 5.7 %psum.7 = f32[512]{0:T(512)S(1)} all-reduce(f32[512]{0:T(512)S(1)} %get-tuple-element.278), channel_id=1, replica_groups=mesh['seq'=8,'grp'=4] {'grp'}, use_global_device_ids=true, to_apply=%region_10.11 | all-reduce | flops 512 | bytes 4096 | tf_op jit(solution)/shard_map/psum | solution.py:156
  469.7 33.1 %all-gather.5.cloned.1.call-done = bf16[512,5120]{0,1:T(8,128)(2,1)} async-done(((bf16[512,1280]{0,1:T(8,128)(2,1)}), bf16[512,5120]{0,1:T(8,128)(2,1)}) %all-gather.5.cloned.1.call-update) | async-done | bytes 5242896 | tf_op jit(solution)/shard_map/all_gather | solution.py:160
  502.7 9.6 %fusion.52 = bf16[512,640]{1,0:T(8,128)(2,1)} fusion(bf16[512,5120]{0,1:T(8,128)(2,1)} %all-gather.5.cloned.1.call-done, bf16[5120,640]{1,0:T(8,128)(2,1)} %param.27, f32[512]{0:T(512)S(1)} %add_rsqrt_fusion), kind=kOutput, calls=%fused_computation.80 | convolution fusion | flops 3356098560 | bytes 12453888 | tf_op jit(solution)/shard_map/dot_general | solution.py:159
  (160 shorter events, 73.4 us)
Async XLA Ops:
  6.5 85.6 %copy-start = (bf16[2560,20]{0,1:T(8,128)(2,1)S(1)}, bf16[2560,20]{0,1:T(8,128)(2,1)}, u32[]{:S(2)}) copy-start(bf16[2560,20]{0,1:T(8,128)(2,1)} %param.20) | copy-start | bytes 307204
  6.5 78.2 %copy-start.6 = (bf16[512,2560]{1,0:T(8,128)(2,1)S(1)}, bf16[512,2560]{1,0:T(8,128)(2,1)}, u32[]{:S(2)}) copy-start(bf16[512,2560]{1,0:T(8,128)(2,1)} %param.16) | copy-start | bytes 7864324
  6.5 441.3 %all-gather.7.cloned.1.call-start = ((), (), s32[]{:S(2)}) async-start(), calls=%async_computation.1 | async-start | bytes 5898240 | tf_op jit(solution)/shard_map/all_gather | solution.py:20
  6.5 73.5 %collective-permute-start = (bf16[2560,2,160]{0,2,1:T(8,128)(2,1)}, bf16[2560,2,160]{0,2,1:T(8,128)(2,1)S(1)}, u32[]{:S(2)}, u32[]{:S(2)}) collective-permute-start(bf16[2560,2,160]{0,2,1:T(8,128)(2,1)} %param.18), channel_id=1, source_target_pairs={{0,4},{4,8},{8,12},{12,16},{16,20},{20,24},{24,28},{28,0},{1,5},{5... | collective-permute-start | bytes 4915208 | tf_op jit(solution)/shard_map/ppermute | solution.py:94
  9.5 80.2 %collective-permute-start.1 = (bf16[2560,2,160]{0,2,1:T(8,128)(2,1)}, bf16[2560,2,160]{0,2,1:T(8,128)(2,1)}, u32[]{:S(2)}, u32[]{:S(2)}) collective-permute-start(bf16[2560,2,160]{0,2,1:T(8,128)(2,1)} %param.18), channel_id=1, source_target_pairs={{0,28},{4,0},{8,4},{12,8},{16,12},{20,16},{24,20},{28,24},{1,29},{... | collective-permute-start | bytes 4915208 | tf_op jit(solution)/shard_map/ppermute | solution.py:99
  80.0 7.0 %copy-start.7 = (bf16[2560,2,160]{0,2,1:T(8,128)(2,1)}, bf16[2560,2,160]{0,2,1:T(8,128)(2,1)S(1)}, u32[]{:S(2)}) copy-start(bf16[2560,2,160]{0,2,1:T(8,128)(2,1)S(1)} %collective-permute-done) | copy-start | bytes 4915204
  80.0 71.7 %collective-permute-start.2 = (bf16[2560,2,160]{0,2,1:T(8,128)(2,1)S(1)}, bf16[2560,2,160]{0,2,1:T(8,128)(2,1)}, u32[]{:S(2)}, u32[]{:S(2)}) collective-permute-start(bf16[2560,2,160]{0,2,1:T(8,128)(2,1)S(1)} %collective-permute-done), channel_id=1, source_target_pairs={{0,4},{4,8},{8,12},{12,16},{16,20},{20,24},{24,28},{28,0},{1,5},{5... | collective-permute-start | bytes 4915208 | tf_op jit(solution)/shard_map/ppermute | solution.py:94
  84.7 4.9 copy-start.16
  84.8 7.4 %copy-start.17 = (f32[2560]{0:T(1024)S(1)}, f32[2560]{0:T(1024)}, u32[]{:S(2)}) copy-start(f32[2560]{0:T(1024)} %param.17) | copy-start | bytes 30724
  84.8 7.4 %copy-start.18 = (f32[20]{0:T(128)S(1)}, f32[20]{0:T(128)}, u32[]{:S(2)}) copy-start(f32[20]{0:T(128)} %param.21) | copy-start | bytes 244
  87.1 67.3 %copy-start.12 = (bf16[4,1280]{1,0:T(4,128)(2,1)S(1)}, bf16[4,1280]{1,0:T(4,128)(2,1)}, u32[]{:S(2)}) copy-start(bf16[4,1280]{1,0:T(4,128)(2,1)} %param.24) | copy-start | bytes 30724
  87.1 76.5 %collective-permute-start.8 = (bf16[3,2,128]{2,0,1:T(4,128)(2,1)S(1)}, bf16[3,2,128]{2,0,1:T(4,128)(2,1)S(1)}, u32[]{:S(2)}, u32[]{:S(2)}) collective-permute-start(bf16[3,2,128]{2,0,1:T(4,128)(2,1)S(1)} %slice_bitcast_fusion.2), channel_id=1, source_target_pairs={{0,4},{4,8},{8,12},{12,16},{16,20},{20,24},{24,28},{1,5},{5,9},{9,... | collective-permute-start | bytes 4616 | tf_op jit(solution)/shard_map/ppermute | solution.py:15
  89.7 76.1 %collective-permute-start.3 = (bf16[2560,2,160]{0,2,1:T(8,128)(2,1)}, bf16[2560,2,160]{0,2,1:T(8,128)(2,1)}, u32[]{:S(2)}, u32[]{:S(2)}) collective-permute-start(bf16[2560,2,160]{0,2,1:T(8,128)(2,1)} %collective-permute-done.1), channel_id=1, source_target_pairs={{0,28},{4,0},{8,4},{12,8},{16,12},{20,16},{24,20},{28,24},{1,29},{... | collective-permute-start | bytes 4915208 | tf_op jit(solution)/shard_map/ppermute | solution.py:99
  151.7 71.3 %collective-permute-start.4 = (bf16[2560,2,160]{0,2,1:T(8,128)(2,1)}, bf16[2560,2,160]{0,2,1:T(8,128)(2,1)}, u32[]{:S(2)}, u32[]{:S(2)}) collective-permute-start(bf16[2560,2,160]{0,2,1:T(8,128)(2,1)} %collective-permute-done.2), channel_id=1, source_target_pairs={{0,4},{4,8},{8,12},{12,16},{16,20},{20,24},{24,28},{28,0},{1,5},{5... | collective-permute-start | bytes 4915208 | tf_op jit(solution)/shard_map/ppermute | solution.py:94
  163.5 5.4 %copy-start.8 = (bf16[2560,2,160]{0,2,1:T(8,128)(2,1)S(1)}, bf16[2560,2,160]{0,2,1:T(8,128)(2,1)}, u32[]{:S(2)}) copy-start(bf16[2560,2,160]{0,2,1:T(8,128)(2,1)} %copy-done.7) | copy-start | bytes 4915204
  165.8 70.6 %collective-permute-start.5 = (bf16[2560,2,160]{0,2,1:T(8,128)(2,1)}, bf16[2560,2,160]{0,2,1:T(8,128)(2,1)S(1)}, u32[]{:S(2)}, u32[]{:S(2)}) collective-permute-start(bf16[2560,2,160]{0,2,1:T(8,128)(2,1)} %collective-permute-done.3), channel_id=1, source_target_pairs={{0,28},{4,0},{8,4},{12,8},{16,12},{20,16},{24,20},{28,24},{1,29},{... | collective-permute-start | bytes 4915208 | tf_op jit(solution)/shard_map/ppermute | solution.py:99
  223.1 38.9 %collective-permute-start.6 = (bf16[2560,2,160]{0,2,1:T(8,128)(2,1)}, bf16[2560,2,160]{0,2,1:T(8,128)(2,1)S(1)}, u32[]{:S(2)}, u32[]{:S(2)}) collective-permute-start(bf16[2560,2,160]{0,2,1:T(8,128)(2,1)} %collective-permute-done.4), channel_id=1, source_target_pairs={{0,4},{4,8},{8,12},{12,16},{16,20},{20,24},{24,28},{28,0},{1,5},{5... | collective-permute-start | bytes 4915208 | tf_op jit(solution)/shard_map/ppermute | solution.py:94
  277.6 5.9 %collective-permute-start.7 = (bf16[3,1280]{0,1:T(8,128)(2,1)S(1)}, bf16[3,1280]{0,1:T(8,128)(2,1)S(1)}, u32[]{:S(2)}, u32[]{:S(2)}) collective-permute-start(bf16[3,1280]{0,1:T(8,128)(2,1)S(1)} %slice_bitcast_fusion.1), channel_id=1, source_target_pairs={{0,4},{4,8},{8,12},{12,16},{16,20},{20,24},{24,28},{1,5},{5,9},{9,... | collective-permute-start | bytes 23048 | tf_op jit(solution)/shard_map/ppermute | solution.py:15
  294.8 28.9 %copy-start.11 = (f32[2,256,20]{1,0,2:T(2,128)S(1)}, f32[2,256,20]{1,0,2:T(2,128)}, u32[]{:S(2)}) copy-start(f32[2,256,20]{1,0,2:T(2,128)} %copy-done.10) | copy-start | bytes 122884 | tf_op jit(solution)/shard_map/while
  330.4 28.9 %copy-start.11 = (f32[2,256,20]{1,0,2:T(2,128)S(1)}, f32[2,256,20]{1,0,2:T(2,128)}, u32[]{:S(2)}) copy-start(f32[2,256,20]{1,0,2:T(2,128)} %copy-done.10) | copy-start | bytes 122884 | tf_op jit(solution)/shard_map/while
  360.2 142.6 %all-gather.5.cloned.1.call-start = ((), (), s32[]{:S(2)}) async-start(), calls=%async_computation | async-start | bytes 6553600 | tf_op jit(solution)/shard_map/all_gather | solution.py:160
  384.7 73.3 %copy-start.5 = (f32[512,1,1280]{0,2,1:T(8,128)S(1)}, f32[512,1,1280]{0,2,1:T(8,128)}, u32[]{:S(2)}) copy-start(f32[512,1,1280]{0,2,1:T(8,128)} %get-tuple-element.268) | copy-start | bytes 7864324
  458.0 4.0 copy-start.4
  502.7 9.6 %copy-start.1 = (bf16[2560,20]{0,1:T(8,128)(2,1)S(1)}, bf16[2560,20]{0,1:T(8,128)(2,1)}, u32[]{:S(2)}) copy-start(bf16[2560,20]{0,1:T(8,128)(2,1)} %param.20) | copy-start | bytes 307204
  (8 other events, 11.8 us)
Sparse Core Ops, SparseCore 0:
  360.3 87.4 all-gather.6
  464.1 38.5 all-gather.4
